TPU v7x, 32 devices: a whole 2x2x4 slice. The times are simulated.
32 devices in a mesh: dp: 2 (over x), fsdp: 4 (over z), mp: 4 (over y, core).
Axes of the slice: x: 2, y: 2, z: 4, core: 2. Of those that a mesh axis runs over, the one named last changes fastest.
Arguments:
- gradients: bfloat16 [8, 12, 2, 256, 1024], P(('dp', 'fsdp'), None, None, None, 'mp'), may hold values from -6 to 6
- master: float32 [12, 2, 256, 1024], P(None, None, ('dp', 'fsdp'), 'mp'), may hold values from -0.375 to 0.375
- teacher: float32 [12, 2, 256, 1024], P(None, None, ('dp', 'fsdp'), 'mp'), may hold values from -0.375 to 0.375
- first_moment: float32 [12, 2, 256, 1024], P(None, None, ('dp', 'fsdp'), 'mp'), may hold values from -2.2888184e-05 to 2.2888184e-05
- second_moment: float32 [12, 2, 256, 1024], P(None, None, ('dp', 'fsdp'), 'mp'), may hold values from 0 to 1, as said below
- layer_rates: float32 [12], replicated, may hold values from 0.02 to 0.2
Outputs:
- master_new: float32 [12, 2, 256, 1024], P(None, None, ('dp', 'fsdp'), 'mp')
- teacher_new: float32 [12, 2, 256, 1024], P(None, None, ('dp', 'fsdp'), 'mp')
- first_new: float32 [12, 2, 256, 1024], P(None, None, ('dp', 'fsdp'), 'mp')
- second_new: float32 [12, 2, 256, 1024], P(None, None, ('dp', 'fsdp'), 'mp')
- student_weights: bfloat16 [12, 2, 256, 1024], P(None, None, None, 'mp')
- teacher_weights: bfloat16 [12, 2, 256, 1024], P(None, None, None, 'mp')
Inputs may be any that keep to these rules, and one draw needn't show every extreme that they name: `second_moment`: every entry is positive.
All inputs are finite; a program needn't handle non-finite values.
Results may differ from a plain program's by a relative error of at most 0.0004.
Values may be sent and summed in bfloat16 or wider, within the bound.
A program may use at most 64 MiB of HBM per device.

v0:
```python
import jax
import jax.numpy as jnp
from jax import lax
from jax.sharding import PartitionSpec as P

CLIP_NORM = 0.1
BETA_ONE = 0.9
BETA_TWO = 0.999
BIAS_ONE = 1.0 - 0.9**50 * 0.9**50
BIAS_TWO = 1.0 - 0.999**50 * 0.999**50
ADAM_EPS = 1e-08
DECAY = 0.05
EMA_KEEP = 0.95


def shards(gradients, master, teacher, first_moment, second_moment, layer_rates):
    own_grad = gradients[0].astype(jnp.float32)
    summed = lax.psum_scatter(own_grad, ("dp", "fsdp"), scatter_dimension=2, tiled=True)
    mean_grad = summed / (lax.axis_size("dp") * lax.axis_size("fsdp"))
    norm_sq = lax.psum(jnp.sum(mean_grad * mean_grad), ("dp", "fsdp", "mp"))
    clip_factor = jnp.minimum(1.0, CLIP_NORM / (jnp.sqrt(norm_sq) + 1e-06))
    clipped = clip_factor * mean_grad
    first_new = BETA_ONE * first_moment + (1.0 - BETA_ONE) * clipped
    second_new = BETA_TWO * second_moment + (1.0 - BETA_TWO) * clipped * clipped
    direction = first_new / BIAS_ONE / (jnp.sqrt(second_new / BIAS_TWO) + ADAM_EPS) + DECAY * master
    layer_rate = layer_rates[:, None, None, None]
    master_new = master - layer_rate * direction
    teacher_new = EMA_KEEP * teacher + (1.0 - EMA_KEEP) * master_new
    student_half = master_new.astype(jnp.bfloat16)
    teacher_half = teacher_new.astype(jnp.bfloat16)
    student_weights, teacher_weights = (
        lax.all_gather(student_half, ("dp", "fsdp"), axis=2, tiled=True),
        lax.all_gather(teacher_half, ("dp", "fsdp"), axis=2, tiled=True),
    )
    return (master_new, teacher_new, first_new, second_new, student_weights, teacher_weights)


def solution(mesh):
    placed = (
        P(("dp", "fsdp"), None, None, None, "mp"),
        P(None, None, ("dp", "fsdp"), "mp"),
        P(None, None, ("dp", "fsdp"), "mp"),
        P(None, None, ("dp", "fsdp"), "mp"),
        P(None, None, ("dp", "fsdp"), "mp"),
        P(),
    )
    return jax.shard_map(
        shards,
        mesh=mesh,
        in_specs=placed,
        out_specs=(
            P(None, None, ("dp", "fsdp"), "mp"),
            P(None, None, ("dp", "fsdp"), "mp"),
            P(None, None, ("dp", "fsdp"), "mp"),
            P(None, None, ("dp", "fsdp"), "mp"),
            P(None, None, None, "mp"),
            P(None, None, None, "mp"),
        ),
        check_vma=False,
    )
```

profile of v0, /device:TPU:0, one launch (start us, length us, event | category | flops | bytes accessed | tf_op | source)
XLA Modules:
  0.0 313.6 jit_solution(9749156798036131048)
XLA Ops:
  7.2 0.0 reduce-scatter.2.cloned.1.call-start
  7.2 5.3 %bitcast_convert_fusion = f32[12,2,256,256]{3,2,1,0:T(8,128)} fusion(bf16[1,12,2,256,256]{4,3,2,1,0:T(8,128)(2,1)} %param.6), kind=kLoop, calls=%fused_computation | loop fusion | flops 1572864 | bytes 9437184 | tf_op jit(solution)/shard_map/convert_element_type | solution.py:17
  12.5 0.0 copy-start.2
  12.5 0.0 copy-start.3
  12.5 0.0 reduce-scatter.2.cloned.1.call-update
  12.6 0.0 all-gather.5.cloned.1.call-start
  12.6 121.3 %reduce-scatter.2.cloned.1.call-done = f32[12,2,32,256]{3,2,1,0:T(8,128)} async-done(((f32[12,2,256,256]{3,2,1,0:T(8,128)}), f32[12,2,32,256]{3,2,1,0:T(8,128)}) %reduce-scatter.2.cloned.1.call-update) | async-done | bytes 786448 | tf_op jit(solution)/shard_map/reduce_scatter | solution.py:18
  133.9 1.9 multiply_reduce_fusion
  135.8 39.7 %psum.7 = f32[]{:T(128)} all-reduce(f32[]{:T(128)} %multiply_reduce_fusion), channel_id=1, replica_groups=mesh['dp'=2,'fsdp'=4,'mp'=4] {'dp','fsdp','mp'}, use_global_device_ids=true, to_apply=%region_2.0 | all-reduce | flops 1 | bytes 8 | tf_op jit(solution)/shard_map/psum | solution.py:20
  176.3 0.0 copy-done.2
  176.3 0.0 copy-done.3
  176.3 0.0 copy-done.4
  176.3 0.0 copy-done.5
  176.3 3.5 %fusion.1 = (bf16[12,2,32,256]{3,2,1,0:T(8,128)(2,1)}, f32[12,2,32,256]{3,2,1,0:T(8,128)}, f32[12,2,32,256]{3,2,1,0:T(8,128)S(1)}, f32[12,2,32,256]{3,2,1,0:T(8,128)}, f32[12,2,32,256]{3,2,1,0:T(8,128)}) fusion(f32[12,2,32,256]{3,2,1,0:T(8,128)S(1)} %copy-done.2, f32[12,2,32,256]{3,2,1,0:T(8,128)S(1)} %copy-done.3, f32[12]{0:T(128)S(1)} %copy-done.5, ...), kind=kLoop, calls=%fused_computation.7 | loop fusion | flops 3932160 | bytes 7471156 | tf_op jit(solution)/shard_map/convert_element_type | solution.py:30
  179.8 0.0 all-gather.5.cloned.1.call-update
  179.8 0.0 all-gather.3.cloned.1.call-start
  179.9 1.0 convert_element_type.14
  180.9 0.0 all-gather.3.cloned.1.call-update
  180.9 59.0 %all-gather.5.cloned.1.call-done = bf16[12,2,256,256]{3,2,1,0:T(8,128)(2,1)} async-done(((bf16[12,2,32,256]{3,2,1,0:T(8,128)(2,1)}), bf16[12,2,256,256]{3,2,1,0:T(8,128)(2,1)}) %all-gather.5.cloned.1.call-update) | async-done | bytes 3145744 | tf_op jit(solution)/shard_map/all_gather | solution.py:33
  239.9 61.5 %all-gather.3.cloned.1.call-done = bf16[12,2,256,256]{3,2,1,0:T(8,128)(2,1)} async-done(((bf16[12,2,32,256]{3,2,1,0:T(8,128)(2,1)}), bf16[12,2,256,256]{3,2,1,0:T(8,128)(2,1)}) %all-gather.3.cloned.1.call-update) | async-done | bytes 3145744 | tf_op jit(solution)/shard_map/all_gather | solution.py:32
  301.4 4.0 %copy.14 = bf16[12,2,256,256]{3,2,1,0:T(8,128)(2,1)} copy(bf16[12,2,256,256]{3,2,1,0:T(8,128)(2,1)} %all-gather.3.cloned.1.call-done) | data formatting | bytes 6291456
  305.4 0.0 copy-done.1
  305.4 0.0 copy-done
  305.4 1.7 copy.15
  (4 shorter events, 0.0 us)
Async XLA Ops:
  7.2 126.7 %reduce-scatter.2.cloned.1.call-start = ((), (), s32[]{:S(2)}) async-start(), calls=%async_computation.1 | async-start | bytes 7077888 | tf_op jit(solution)/shard_map/reduce_scatter | solution.py:18
  12.5 163.8 %copy-start.2 = (f32[12,2,32,256]{3,2,1,0:T(8,128)S(1)}, f32[12,2,32,256]{3,2,1,0:T(8,128)}, u32[]{:S(2)}) copy-start(f32[12,2,32,256]{3,2,1,0:T(8,128)} %param.8) | copy-start | bytes 2359300
  12.5 163.8 %copy-start.3 = (f32[12,2,32,256]{3,2,1,0:T(8,128)S(1)}, f32[12,2,32,256]{3,2,1,0:T(8,128)}, u32[]{:S(2)}) copy-start(f32[12,2,32,256]{3,2,1,0:T(8,128)} %param.7) | copy-start | bytes 2359300
  12.5 163.8 %copy-start.4 = (f32[12,2,32,256]{3,2,1,0:T(8,128)S(1)}, f32[12,2,32,256]{3,2,1,0:T(8,128)}, u32[]{:S(2)}) copy-start(f32[12,2,32,256]{3,2,1,0:T(8,128)} %param.9) | copy-start | bytes 2359300
  12.5 163.8 %copy-start.5 = (f32[12]{0:T(128)S(1)}, f32[12]{0:T(128)}, u32[]{:S(2)}) copy-start(f32[12]{0:T(128)} %param.11) | copy-start | bytes 148
  12.6 227.4 %all-gather.5.cloned.1.call-start = ((), (), s32[]{:S(2)}) async-start(), calls=%async_computation.3 | async-start | bytes 3538944 | tf_op jit(solution)/shard_map/all_gather | solution.py:33
  179.8 125.6 %copy-start.1 = (f32[12,2,32,256]{3,2,1,0:T(8,128)}, f32[12,2,32,256]{3,2,1,0:T(8,128)S(1)}, u32[]{:S(2)}) copy-start(f32[12,2,32,256]{3,2,1,0:T(8,128)S(1)} %get-tuple-element.17) | copy-start | bytes 2359300
  179.8 121.6 %all-gather.3.cloned.1.call-start = ((), (), s32[]{:S(2)}) async-start(), calls=%async_computation.2 | async-start | bytes 3538944 | tf_op jit(solution)/shard_map/all_gather | solution.py:32
  301.4 4.0 %copy-start = (bf16[12,2,256,256]{3,2,1,0:T(8,128)(2,1)S(1)}, bf16[12,2,256,256]{3,2,1,0:T(8,128)(2,1)}, u32[]{:S(2)}) copy-start(bf16[12,2,256,256]{3,2,1,0:T(8,128)(2,1)} %all-gather.5.cloned.1.call-done) | copy-start | bytes 9437188
Sparse Core Ops, SparseCore 0:
  12.7 121.1 reduce-scatter.1
  180.0 59.9 all-gather.4
  242.7 58.6 all-gather.2
where the time goes:
time: 314 us
  waiting for transfers between devices  242 us (77%)
  blocking collectives  39.7 us (13%)
  between operations  14.5 us (5%)
  other arithmetic  11.7 us (4%)
  local copies, waits for them, and re-layouts  5.69 us (2%)
    reduce_scatter x1, waiting for transfers between devices, shards(): lax.psum_scatter(own_grad, ('dp', 'fsdp'), scatter_dimension=2, tiled=True)  121 us
    all_gather x1, waiting for transfers between devices, shards(): lax.all_gather(student_half, ('dp', 'fsdp'), axis=2, tiled=True)  61.5 us
    all_gather x1, waiting for transfers between devices, shards(): lax.all_gather(teacher_half, ('dp', 'fsdp'), axis=2, tiled=True)  59 us
    psum x1, blocking collectives, shards(): norm_sq = lax.psum(jnp.sum(mean_grad * mean_grad), ('dp', 'fsdp', 'mp'))  39.7 us
  transfers between devices with their start and end apart: 3, of which 3 were waited for; matrix products, arithmetic and copies ran while one was open for 0% of the time, Pallas kernels for 0%

commit v1 on v0

--- a/solution.py
+++ b/solution.py
@@ -11,6 +11,27 @@
 ADAM_EPS = 1e-08
 DECAY = 0.05
 EMA_KEEP = 0.95
+
+
+def collect(shard, axis, dim):
+    devices, index, rows = (lax.axis_size(axis), lax.axis_index(axis), shard.shape[dim])
+    right = [(i, (i + 1) % devices) for i in range(devices)]
+    left = [(i, (i - 1) % devices) for i in range(devices)]
+    whole = jnp.zeros((*shard.shape[:dim], devices * rows, *shard.shape[dim + 1 :]), shard.dtype)
+    whole = lax.dynamic_update_slice_in_dim(whole, shard, index * rows, axis=dim)
+    from_left = from_right = shard
+    half = devices // 2
+    for step in range(1, half + 1):
+        from_left = lax.ppermute(from_left, axis, right)
+        whole = lax.dynamic_update_slice_in_dim(
+            whole, from_left, (index - step) % devices * rows, axis=dim
+        )
+        if step < devices - half:
+            from_right = lax.ppermute(from_right, axis, left)
+            whole = lax.dynamic_update_slice_in_dim(
+                whole, from_right, (index + step) % devices * rows, axis=dim
+            )
+    return whole
 
 
 def shards(gradients, master, teacher, first_moment, second_moment, layer_rates):
@@ -29,7 +50,7 @@
     student_half = master_new.astype(jnp.bfloat16)
     teacher_half = teacher_new.astype(jnp.bfloat16)
     student_weights, teacher_weights = (
-        lax.all_gather(student_half, ("dp", "fsdp"), axis=2, tiled=True),
+        collect(student_half, ("dp", "fsdp"), 2),
         lax.all_gather(teacher_half, ("dp", "fsdp"), axis=2, tiled=True),
     )
     return (master_new, teacher_new, first_new, second_new, student_weights, teacher_weights)

time: 314 us -> 295 us (0.939)
  waiting for transfers between devices: 242 us -> 213 us
  starting transfers between devices: 0.12 us -> 5.72 us
  local copies, waits for them, and re-layouts: 5.69 us -> 10.3 us
    ppermute x0 -> x7, waiting for transfers between devices: none -> 91.6 us  [the longest x3 59.4 us: collect(): from_right = lax.ppermute(from_right, axis, left)]
    all_gather x1 -> x0, waiting for transfers between devices: 61.5 us -> none  [shards(): lax.all_gather(student_half, ('dp', 'fsdp'), axis=2, tiled=True)]
    all_gather x1, waiting for transfers between devices: 59 us -> 0.02 us  [shards(): lax.all_gather(teacher_half, ('dp', 'fsdp'), axis=2, tiled=True)]
    ppermute x0 -> x7, starting transfers between devices: none -> 5.64 us  [the longest x3 3.66 us: collect(): from_right = lax.ppermute(from_right, axis, left)]
    dynamic_update_slice x0 -> x7, local copies, waits for them, and re-layouts: none -> 4.21 us  [the longest x4 2.12 us: collect(): lax.dynamic_update_slice_in_dim(whole, from_left, (index - step) % device...]
  transfers between devices with their start and end apart: 3 -> 9, of which waited for: 3 -> 8; matrix products, arithmetic and copies ran while one was open for 0% -> 2% of each run, Pallas kernels for 0% -> 0%
where the time goes in v1:
time: 295 us
  waiting for transfers between devices  213 us (72%)
  blocking collectives  39.7 us (13%)
  between operations  14.9 us (5%)
  other arithmetic  10.8 us (4%)
  local copies, waits for them, and re-layouts  10.3 us (3%)
  starting transfers between devices  5.72 us (2%)
    reduce_scatter x1, waiting for transfers between devices, shards(): lax.psum_scatter(own_grad, ('dp', 'fsdp'), scatter_dimension=2, tiled=True)  121 us
    ppermute x3, waiting for transfers between devices, collect(): from_right = lax.ppermute(from_right, axis, left)  59.4 us
    psum x1, blocking collectives, shards(): norm_sq = lax.psum(jnp.sum(mean_grad * mean_grad), ('dp', 'fsdp', 'mp'))  39.7 us
    ppermute x4, waiting for transfers between devices, collect(): from_left = lax.ppermute(from_left, axis, right)  32.3 us
  transfers between devices with their start and end apart: 9, of which 8 were waited for; matrix products, arithmetic and copies ran while one was open for 2% of the time, Pallas kernels for 0%

profile of v1, /device:TPU:0, one launch (start us, length us, event | category | flops | bytes accessed | tf_op | source)
XLA Modules:
  0.0 294.5 jit_solution(7379937377530156153)
XLA Ops:
  7.2 5.3 %bitcast_convert_fusion = f32[12,2,256,256]{3,2,1,0:T(8,128)} fusion(bf16[1,12,2,256,256]{4,3,2,1,0:T(8,128)(2,1)} %param.6), kind=kLoop, calls=%fused_computation | loop fusion | flops 1572864 | bytes 9437184 | tf_op jit(solution)/shard_map/convert_element_type | solution.py:38
  12.6 0.0 all-gather.2.cloned.1.call-start
  12.6 121.3 %reduce-scatter.2.cloned.1.call-done = f32[12,2,32,256]{3,2,1,0:T(8,128)} async-done(((f32[12,2,256,256]{3,2,1,0:T(8,128)}), f32[12,2,32,256]{3,2,1,0:T(8,128)}) %reduce-scatter.2.cloned.1.call-update) | async-done | bytes 786448 | tf_op jit(solution)/shard_map/reduce_scatter | solution.py:39
  133.9 1.9 multiply_reduce_fusion
  135.8 39.7 %psum.7 = f32[]{:T(128)} all-reduce(f32[]{:T(128)} %multiply_reduce_fusion), channel_id=1, replica_groups=mesh['dp'=2,'fsdp'=4,'mp'=4] {'dp','fsdp','mp'}, use_global_device_ids=true, to_apply=%region_2.0 | all-reduce | flops 1 | bytes 8 | tf_op jit(solution)/shard_map/psum | solution.py:41
  176.3 3.5 %fusion.1 = (bf16[12,2,32,256]{3,2,1,0:T(8,128)(2,1)}, f32[12,2,32,256]{3,2,1,0:T(8,128)}, f32[12,2,32,256]{3,2,1,0:T(8,128)}, f32[12,2,32,256]{3,2,1,0:T(8,128)}, f32[12,2,32,256]{3,2,1,0:T(8,128)}) fusion(f32[12,2,32,256]{3,2,1,0:T(8,128)S(1)} %copy-done.2, f32[12,2,32,256]{3,2,1,0:T(8,128)S(1)} %copy-done.3, f32[12]{0:T(128)S(1)} %copy-done.7, ...), kind=kLoop, calls=%fused_computation.15 | loop fusion | flops 3932160 | bytes 7471156 | tf_op jit(solution)/shard_map/convert_element_type | solution.py:51
  179.9 0.3 broadcast_in_dim.4
  180.2 0.8 copy-done.1
  181.0 0.1 constant_dynamic-update-slice_fusion.7
  181.1 1.1 collective-permute-start
  182.2 3.7 %collective-permute-start.1 = (bf16[12,2,32,256]{3,2,1,0:T(8,128)(2,1)S(1)}, bf16[12,2,32,256]{3,2,1,0:T(8,128)(2,1)}, u32[]{:S(2)}, u32[]{:S(2)}) collective-permute-start(bf16[12,2,32,256]{3,2,1,0:T(8,128)(2,1)S(1)} %get-tuple-element.12), channel_id=1, source_target_pairs={{0,28},{4,0},{8,4},{12,8},{16,12},{20,16},{24,20},{28,24},{1,29},{... | collective-permute-start | bytes 1179656 | tf_op jit(solution)/shard_map/ppermute | solution.py:30
  185.9 12.2 %collective-permute-done = bf16[12,2,32,256]{3,2,1,0:T(8,128)(2,1)S(1)} collective-permute-done((bf16[12,2,32,256]{3,2,1,0:T(8,128)(2,1)S(1)}, bf16[12,2,32,256]{3,2,1,0:T(8,128)(2,1)S(1)}, u32[]{:S(2)}, u32[]{:S(2)}) %collective-permute-start) | collective-permute-done | bytes 393248 | tf_op jit(solution)/shard_map/ppermute | solution.py:25
  198.1 19.4 %collective-permute-done.1 = bf16[12,2,32,256]{3,2,1,0:T(8,128)(2,1)} collective-permute-done((bf16[12,2,32,256]{3,2,1,0:T(8,128)(2,1)S(1)}, bf16[12,2,32,256]{3,2,1,0:T(8,128)(2,1)}, u32[]{:S(2)}, u32[]{:S(2)}) %collective-permute-start.1) | collective-permute-done | bytes 393248 | tf_op jit(solution)/shard_map/ppermute | solution.py:30
  217.4 8.0 %collective-permute-done.2 = bf16[12,2,32,256]{3,2,1,0:T(8,128)(2,1)} collective-permute-done((bf16[12,2,32,256]{3,2,1,0:T(8,128)(2,1)S(1)}, bf16[12,2,32,256]{3,2,1,0:T(8,128)(2,1)}, u32[]{:S(2)}, u32[]{:S(2)}) %collective-permute-start.2) | collective-permute-done | bytes 393248 | tf_op jit(solution)/shard_map/ppermute | solution.py:25
  225.5 1.0 constant_dynamic-update-slice_fusion.6
  226.5 24.8 %collective-permute-done.3 = bf16[12,2,32,256]{3,2,1,0:T(8,128)(2,1)} collective-permute-done((bf16[12,2,32,256]{3,2,1,0:T(8,128)(2,1)}, bf16[12,2,32,256]{3,2,1,0:T(8,128)(2,1)}, u32[]{:S(2)}, u32[]{:S(2)}) %collective-permute-start.3) | collective-permute-done | bytes 393248 | tf_op jit(solution)/shard_map/ppermute | solution.py:30
  251.3 1.0 constant_dynamic-update-slice_fusion.5
  252.3 4.0 %collective-permute-done.4 = bf16[12,2,32,256]{3,2,1,0:T(8,128)(2,1)S(1)} collective-permute-done((bf16[12,2,32,256]{3,2,1,0:T(8,128)(2,1)}, bf16[12,2,32,256]{3,2,1,0:T(8,128)(2,1)S(1)}, u32[]{:S(2)}, u32[]{:S(2)}) %collective-permute-start.4) | collective-permute-done | bytes 393248 | tf_op jit(solution)/shard_map/ppermute | solution.py:25
  256.4 0.9 collective-permute-start.6
  257.2 1.0 constant_dynamic-update-slice_fusion.4
  258.3 1.0 constant_dynamic-update-slice_fusion.3
  259.3 15.2 %collective-permute-done.5 = bf16[12,2,32,256]{3,2,1,0:T(8,128)(2,1)S(1)} collective-permute-done((bf16[12,2,32,256]{3,2,1,0:T(8,128)(2,1)}, bf16[12,2,32,256]{3,2,1,0:T(8,128)(2,1)S(1)}, u32[]{:S(2)}, u32[]{:S(2)}) %collective-permute-start.5) | collective-permute-done | bytes 393248 | tf_op jit(solution)/shard_map/ppermute | solution.py:30
  274.6 8.1 %collective-permute-done.6 = bf16[12,2,32,256]{3,2,1,0:T(8,128)(2,1)S(1)} collective-permute-done((bf16[12,2,32,256]{3,2,1,0:T(8,128)(2,1)S(1)}, bf16[12,2,32,256]{3,2,1,0:T(8,128)(2,1)S(1)}, u32[]{:S(2)}, u32[]{:S(2)}) %collective-permute-start.6) | collective-permute-done | bytes 393248 | tf_op jit(solution)/shard_map/ppermute | solution.py:25
  282.7 5.0 %copy.21 = bf16[12,2,256,256]{3,2,1,0:T(8,128)(2,1)} copy(bf16[12,2,256,256]{3,2,1,0:T(8,128)(2,1)} %all-gather.2.cloned.1.call-done) | data formatting | bytes 6291456
  (26 shorter events, 0.2 us)
Async XLA Ops:
  7.2 126.7 %reduce-scatter.2.cloned.1.call-start = ((), (), s32[]{:S(2)}) async-start(), calls=%async_computation.1 | async-start | bytes 7077888 | tf_op jit(solution)/shard_map/reduce_scatter | solution.py:39
  12.5 163.8 %copy-start.2 = (f32[12,2,32,256]{3,2,1,0:T(8,128)S(1)}, f32[12,2,32,256]{3,2,1,0:T(8,128)}, u32[]{:S(2)}) copy-start(f32[12,2,32,256]{3,2,1,0:T(8,128)} %param.8) | copy-start | bytes 2359300
  12.5 163.8 %copy-start.3 = (f32[12,2,32,256]{3,2,1,0:T(8,128)S(1)}, f32[12,2,32,256]{3,2,1,0:T(8,128)}, u32[]{:S(2)}) copy-start(f32[12,2,32,256]{3,2,1,0:T(8,128)} %param.7) | copy-start | bytes 2359300
  12.5 163.8 %copy-start.4 = (f32[12,2,32,256]{3,2,1,0:T(8,128)S(1)}, f32[12,2,32,256]{3,2,1,0:T(8,128)}, u32[]{:S(2)}) copy-start(f32[12,2,32,256]{3,2,1,0:T(8,128)} %param.9) | copy-start | bytes 2359300
  12.5 163.8 %copy-start.5 = (f32[12,2,32,256]{3,2,1,0:T(8,128)S(1)}, f32[12,2,32,256]{3,2,1,0:T(8,128)}, u32[]{:S(2)}) copy-start(f32[12,2,32,256]{3,2,1,0:T(8,128)} %param.10) | copy-start | bytes 2359300
  12.5 163.8 %copy-start.7 = (f32[12]{0:T(128)S(1)}, f32[12]{0:T(128)}, u32[]{:S(2)}) copy-start(f32[12]{0:T(128)} %param.11) | copy-start | bytes 148
  12.6 270.1 %all-gather.2.cloned.1.call-start = ((), (), s32[]{:S(2)}) async-start(), calls=%async_computation.2 | async-start | bytes 3538944 | tf_op jit(solution)/shard_map/all_gather | solution.py:54
  179.9 1.1 copy-start.1
  181.1 16.9 %collective-permute-start = (bf16[12,2,32,256]{3,2,1,0:T(8,128)(2,1)S(1)}, bf16[12,2,32,256]{3,2,1,0:T(8,128)(2,1)S(1)}, u32[]{:S(2)}, u32[]{:S(2)}) collective-permute-start(bf16[12,2,32,256]{3,2,1,0:T(8,128)(2,1)S(1)} %get-tuple-element.12), channel_id=1, source_target_pairs={{0,4},{4,8},{8,12},{12,16},{16,20},{20,24},{24,28},{28,0},{1,5},{5... | collective-permute-start | bytes 1179656 | tf_op jit(solution)/shard_map/ppermute | solution.py:25
  182.2 35.2 %collective-permute-start.1 = (bf16[12,2,32,256]{3,2,1,0:T(8,128)(2,1)S(1)}, bf16[12,2,32,256]{3,2,1,0:T(8,128)(2,1)}, u32[]{:S(2)}, u32[]{:S(2)}) collective-permute-start(bf16[12,2,32,256]{3,2,1,0:T(8,128)(2,1)S(1)} %get-tuple-element.12), channel_id=1, source_target_pairs={{0,28},{4,0},{8,4},{12,8},{16,12},{20,16},{24,20},{28,24},{1,29},{... | collective-permute-start | bytes 1179656 | tf_op jit(solution)/shard_map/ppermute | solution.py:30
  198.0 19.4 %copy-start.6 = (bf16[12,2,32,256]{3,2,1,0:T(8,128)(2,1)}, bf16[12,2,32,256]{3,2,1,0:T(8,128)(2,1)S(1)}, u32[]{:S(2)}) copy-start(bf16[12,2,32,256]{3,2,1,0:T(8,128)(2,1)S(1)} %collective-permute-done) | copy-start | bytes 1179652
  198.0 27.4 %collective-permute-start.2 = (bf16[12,2,32,256]{3,2,1,0:T(8,128)(2,1)S(1)}, bf16[12,2,32,256]{3,2,1,0:T(8,128)(2,1)}, u32[]{:S(2)}, u32[]{:S(2)}) collective-permute-start(bf16[12,2,32,256]{3,2,1,0:T(8,128)(2,1)S(1)} %collective-permute-done), channel_id=1, source_target_pairs={{0,4},{4,8},{8,12},{12,16},{16,20},{20,24},{24,28},{28,0},{1,5},{5... | collective-permute-start | bytes 1179656 | tf_op jit(solution)/shard_map/ppermute | solution.py:25
  217.4 33.9 %collective-permute-start.3 = (bf16[12,2,32,256]{3,2,1,0:T(8,128)(2,1)}, bf16[12,2,32,256]{3,2,1,0:T(8,128)(2,1)}, u32[]{:S(2)}, u32[]{:S(2)}) collective-permute-start(bf16[12,2,32,256]{3,2,1,0:T(8,128)(2,1)} %collective-permute-done.1), channel_id=1, source_target_pairs={{0,28},{4,0},{8,4},{12,8},{16,12},{20,16},{24,20},{28,24},{1,29},{... | collective-permute-start | bytes 1179656 | tf_op jit(solution)/shard_map/ppermute | solution.py:30
  225.5 30.9 %collective-permute-start.4 = (bf16[12,2,32,256]{3,2,1,0:T(8,128)(2,1)}, bf16[12,2,32,256]{3,2,1,0:T(8,128)(2,1)S(1)}, u32[]{:S(2)}, u32[]{:S(2)}) collective-permute-start(bf16[12,2,32,256]{3,2,1,0:T(8,128)(2,1)} %collective-permute-done.2), channel_id=1, source_target_pairs={{0,4},{4,8},{8,12},{12,16},{16,20},{20,24},{24,28},{28,0},{1,5},{5... | collective-permute-start | bytes 1179656 | tf_op jit(solution)/shard_map/ppermute | solution.py:25
  251.3 23.2 %collective-permute-start.5 = (bf16[12,2,32,256]{3,2,1,0:T(8,128)(2,1)}, bf16[12,2,32,256]{3,2,1,0:T(8,128)(2,1)S(1)}, u32[]{:S(2)}, u32[]{:S(2)}) collective-permute-start(bf16[12,2,32,256]{3,2,1,0:T(8,128)(2,1)} %collective-permute-done.3), channel_id=1, source_target_pairs={{0,28},{4,0},{8,4},{12,8},{16,12},{20,16},{24,20},{28,24},{1,29},{... | collective-permute-start | bytes 1179656 | tf_op jit(solution)/shard_map/ppermute | solution.py:30
  256.4 26.2 %collective-permute-start.6 = (bf16[12,2,32,256]{3,2,1,0:T(8,128)(2,1)S(1)}, bf16[12,2,32,256]{3,2,1,0:T(8,128)(2,1)S(1)}, u32[]{:S(2)}, u32[]{:S(2)}) collective-permute-start(bf16[12,2,32,256]{3,2,1,0:T(8,128)(2,1)S(1)} %collective-permute-done.4), channel_id=1, source_target_pairs={{0,4},{4,8},{8,12},{12,16},{16,20},{20,24},{24,28},{28,0},{1,5},{5... | collective-permute-start | bytes 1179656 | tf_op jit(solution)/shard_map/ppermute | solution.py:25
  282.7 5.0 %copy-start = (bf16[12,2,256,256]{3,2,1,0:T(8,128)(2,1)}, bf16[12,2,256,256]{3,2,1,0:T(8,128)(2,1)S(1)}, u32[]{:S(2)}) copy-start(bf16[12,2,256,256]{3,2,1,0:T(8,128)(2,1)S(1)} %constant_dynamic-update-slice_fusion) | copy-start | bytes 9437188
Sparse Core Ops, SparseCore 0:
  12.7 121.1 reduce-scatter.1
  180.0 93.7 all-gather.1
